TPU v7x, 256 devices: a whole 4x4x8 slice. The times are simulated.
256 devices in a mesh: rel: 8 (over x, core), dst: 16 (over z, y_lo), mp: 2 (over y_hi).
Axes of the slice: x: 4, y: 4 (y_hi: 2, y_lo: 2; y = y_hi * 2 + y_lo), z: 8, core: 2. Of those that a mesh axis runs over, the one named last changes fastest.
Arguments:
- node_table: bfloat16 [131072, 512], P(('rel', 'dst')), may hold values from -6 to 6
- edge_weights: bfloat16 [8, 512, 128, 128], P('rel', 'dst'), may hold values from -0.5 to 0.5
- src_ids: int32 [8, 512, 128], P('rel', 'dst'), may hold values from 0 to 1023
- dst_ids: int32 [8, 512, 128], P('rel', 'dst'), may hold values from 0 to 1023
- block_mask: int32 [8, 512], P('rel', 'dst'), may hold values 0 or 1
- basis_coef: float32 [8, 32], P('rel'), may hold values from -0.1875 to 0.1875
- basis_mats: bfloat16 [32, 512, 512], P(None, None, 'mp'), may hold values from -0.25 to 0.25
- type_bias: float32 [4, 512], P(None, 'mp'), may hold values from -3 to 3
- type_rows: int32 [4], replicated, may hold values from 1 to 512, 1024 in all
- cotangent: bfloat16 [16384, 512], P(('rel', 'dst'), 'mp'), may hold values from -0.0014648438 to 0.0014648438
Outputs:
- layer_out: bfloat16 [16384, 512], P(('rel', 'dst'), 'mp')
- coef_grad: float32 [8, 32], P('rel')
Inputs may be any that keep to these rules, and one draw needn't show every extreme that they name: `type_rows`: the 4 counts sum to 1024.
All inputs are finite; a program needn't handle non-finite values. No bound on the sum of `block_mask` on one device may be relied on, other than what follows from the above.
Results may differ from a plain program's by a relative error of at most 0.0062.
Values may be sent and summed in bfloat16 or wider, within the bound.
A program may use at most 64 MiB of HBM per device.

v0:
```python
import jax
import jax.numpy as jnp
from jax import lax
from jax.sharding import PartitionSpec as P

highest = lax.Precision.HIGHEST


def copy_for_each(x, axis):
    devices = lax.axis_size(axis)
    return lax.all_to_all(jnp.broadcast_to(x[None], (devices, *x.shape)), axis, 0, 0, tiled=True)


def joined_along(tiles, dim):
    tiles = jnp.moveaxis(tiles, 0, dim)
    dims = tiles.shape
    return tiles.reshape(*dims[:dim], dims[dim] * dims[dim + 1], *dims[dim + 2 :])


def gathered_copies(x, axis, dim):
    tiles = copy_for_each(x, axis)
    return joined_along(tiles, dim)


def cut_along(x, dim, devices):
    dims = x.shape
    tiles = x.reshape(*dims[:dim], devices, dims[dim] // devices, *dims[dim + 1 :])
    return jnp.moveaxis(tiles, dim, 0)


def summed_on_arrival(x, axis, dim):
    devices = lax.axis_size(axis)
    tiles = lax.all_to_all(cut_along(x, dim, devices), axis, 0, 0, tiled=True)
    return jnp.sum(tiles, axis=0)


def of_everyone(x, axis):
    return copy_for_each(x, axis).sum(axis=0)


def on_device(
    node_table,
    edge_weights,
    src_ids,
    dst_ids,
    block_mask,
    basis_coef,
    basis_mats,
    type_bias,
    type_rows,
    cotangent,
):
    features = node_table.shape[1]
    out_cols = basis_mats.shape[2]
    basis_count = basis_mats.shape[0]
    block_count = edge_weights.shape[1]
    block_rows = edge_weights.shape[2]
    local_rows = cotangent.shape[0]
    owner_span = local_rows * lax.axis_size("rel")
    contract_rows = (((0,), (0,)), ((), ()))
    picked = jnp.take(node_table, src_ids[0].reshape(-1), axis=0).reshape(
        block_count, block_rows, features
    )
    scaled = edge_weights[0] * block_mask[0][:, None, None].astype(jnp.bfloat16)
    messages = jnp.einsum(
        "kij,kjf->kif", scaled, picked, preferred_element_type=jnp.float32
    ).astype(jnp.bfloat16)
    flat_messages = messages.reshape(-1, features)
    basis_flat = basis_mats.reshape(basis_count, -1)
    mixing = jnp.dot(basis_coef[0], basis_flat, precision=highest)
    weight = mixing.reshape(features, out_cols).astype(jnp.bfloat16)
    owner_grad = gathered_copies(cotangent, "rel", 0)
    slot_local = dst_ids[0]
    outgoing = jnp.dot(flat_messages, weight, preferred_element_type=jnp.float32).astype(
        jnp.bfloat16
    )
    outgoing = outgoing.reshape(block_count, block_rows, out_cols)
    arrived, arrived_ids = (
        lax.all_to_all(outgoing, "dst", split_axis=0, concat_axis=0, tiled=True),
        lax.all_to_all(slot_local, "dst", split_axis=0, concat_axis=0, tiled=True),
    )
    selector = (
        jnp.arange(owner_span, dtype=jnp.int32)[:, None] == arrived_ids.reshape(1, -1)
    ).astype(jnp.bfloat16)
    summed = jnp.dot(selector, arrived.reshape(-1, out_cols), preferred_element_type=jnp.float32)
    wanted = lax.dot_general(
        selector, owner_grad, contract_rows, preferred_element_type=jnp.float32
    ).astype(jnp.bfloat16)
    returned = lax.all_to_all(
        wanted.reshape(block_count, block_rows, out_cols),
        "dst",
        split_axis=0,
        concat_axis=0,
        tiled=True,
    )
    outer_sum = lax.dot_general(
        flat_messages,
        returned.reshape(-1, out_cols),
        contract_rows,
        preferred_element_type=jnp.float32,
    )
    relation_total = summed_on_arrival(summed, "rel", 0)
    position = lax.axis_index("rel") * local_rows + jnp.arange(local_rows, dtype=jnp.int32)
    bounds = jnp.cumsum(type_rows)
    row_kind = jnp.sum((position[:, None] >= bounds[None, :]).astype(jnp.int32), axis=1)
    kind_table = (
        row_kind[:, None] == jnp.arange(type_rows.shape[0], dtype=jnp.int32)[None, :]
    ).astype(jnp.float32)
    row_bias = jnp.dot(kind_table, type_bias, precision=highest)
    layer_out = (relation_total + row_bias).astype(jnp.bfloat16)
    partial_value = jnp.dot(basis_flat, outer_sum.reshape(-1), precision=highest)
    basis_grads = of_everyone(partial_value, ("dst", "mp"))
    return (layer_out, basis_grads[None, :])


def solution(mesh):
    in_specs = (
        P(("rel", "dst"), None),
        P("rel", "dst", None, None),
        P("rel", "dst", None),
        P("rel", "dst", None),
        P("rel", "dst"),
        P("rel", None),
        P(None, None, "mp"),
        P(None, "mp"),
        P(),
        P(("rel", "dst"), "mp"),
    )
    out_specs = (P(("rel", "dst"), "mp"), P("rel", None))
    return jax.shard_map(
        on_device, mesh=mesh, in_specs=in_specs, out_specs=out_specs, check_vma=False
    )
```

profile of v0, /device:TPU:6, one launch (start us, length us, event | category | flops | bytes accessed | tf_op | source)
XLA Modules:
  0.0 183.8 jit_solution(8718821229838077856)
XLA Ops:
  0.6 0.0 copy-start
  0.6 18.3 %all_to_all.35 = s32[16,2,128]{2,1,0:T(2,128)S(1)} all-to-all(s32[16,2,128]{2,1,0:T(2,128)} %bitcast.61), channel_id=1, replica_groups=mesh['rel'=8,'dst'=16,'mp'=2] {'dst'}, dimensions={0} | all-to-all | bytes 32768 | tf_op jit(solution)/shard_map/all_to_all | solution.py:80
  18.9 0.9 broadcast_in_dim.18
  19.8 12.9 %all_to_all.36 = bf16[8,128,256]{2,1,0:T(8,128)(2,1)S(1)} all-to-all(bf16[8,128,256]{2,1,0:T(8,128)(2,1)S(1)} %broadcast_in_dim.18), channel_id=1, replica_groups=mesh['rel'=8,'dst'=16,'mp'=2] {'rel'}, dimensions={0} | all-to-all | bytes 1048576 | tf_op jit(solution)/shard_map/all_to_all | solution.py:11
  32.7 5.9 %fusion.11 = bf16[4096,256]{1,0:T(8,128)(2,1)} fusion(bf16[1024,256]{1,0:T(8,128)(2,1)S(1)} %bitcast.57, s32[4096]{0:T(1024)S(1)} %bitcast.62), kind=kOutput, calls=%fused_computation.13 | convolution fusion | flops 2152726528 | bytes 2637824 | tf_op jit(solution)/shard_map/dot_general | solution.py:86
  38.5 4.0 %all-to-all-start.4 = ((bf16[32,128,256]{2,1,0:T(8,128)(2,1)}), bf16[32,128,256]{2,1,0:T(8,128)(2,1)S(1)}, u32[]{:S(2)}, u32[]{:S(2)}) async-start(bf16[32,128,256]{2,1,0:T(8,128)(2,1)} %bitcast.55), calls=%async_computation.4 | async-start | bytes 4194304 | tf_op jit(solution)/shard_map/all_to_all | solution.py:89
  42.6 0.0 copy-done.2
  42.6 0.0 copy-start.4
  42.7 17.3 %gather_fusion = bf16[4096,512]{1,0:T(8,128)(2,1)} fusion(bf16[1024,512]{1,0:T(8,128)(2,1)S(1)} %copy-done, s32[4096]{0:T(1024)S(1)} %broadcast_clamp_fusion), kind=kCustom, calls=%fused_computation | custom fusion | bytes 8404992 | tf_op jit(solution)/shard_map/jit(_take)/gather | solution.py:61
  59.9 0.0 copy-start.5
  60.0 3.8 %fusion.15 = bf16[32,128,512]{2,1,0:T(8,128)(2,1)S(1)} fusion(bf16[32,128,512]{2,1,0:T(8,128)(2,1)} %bitcast.53, pred[32,128]{1,0:T(8,128)(4,1)S(1)} %compare_and_fusion, bf16[1,32,128,128]{3,2,1,0:T(8,128)(2,1)} %param.11, bf16[32]{0:T(256)(128)(2,1)S(1)} %convert_bitcast_fusion), kind=kOutput, calls=%fused_computation.18 | convolution fusion | flops 541589504 | bytes 9441344 | tf_op jit(solution)/shard_map/kij,kjf->kif/dot_general | solution.py:65
  63.8 13.0 %fusion.3 = bf16[1,512,256]{2,0,1:T(2,128)(2,1)S(1)} fusion(f32[1,32]{1,0:T(1,128)S(1)} %copy-done.5, bf16[4,8,512,256]{3,2,1,0:T(8,128)(2,1)} %bitcast.65), kind=kOutput, calls=%fused_computation.5 | convolution fusion | flops 50331648 | bytes 8650880 | tf_op jit(solution)/shard_map/dot_general | solution.py:70
  76.8 2.6 %convolution_convert_fusion = bf16[4096,256]{1,0:T(8,128)(2,1)} fusion(bf16[4096,512]{1,0:T(8,128)(2,1)S(1)} %bitcast.54, bf16[1,512,256]{2,0,1:T(2,128)(2,1)S(1)} %fusion.3), kind=kOutput, calls=%fused_computation.14 | convolution fusion | flops 1074790400 | bytes 6553600 | tf_op jit(solution)/shard_map/dot_general | solution.py:74
  79.4 13.4 %all-to-all-done.4 = bf16[32,128,256]{2,1,0:T(8,128)(2,1)S(1)} async-done(((bf16[32,128,256]{2,1,0:T(8,128)(2,1)}), bf16[32,128,256]{2,1,0:T(8,128)(2,1)S(1)}, u32[]{:S(2)}, u32[]{:S(2)}) %all-to-all-start.4) | async-done | bytes 2097184 | tf_op jit(solution)/shard_map/all_to_all | solution.py:89
  92.8 4.7 %all-to-all-start.1 = ((bf16[32,128,256]{2,1,0:T(8,128)(2,1)}), bf16[32,128,256]{2,1,0:T(8,128)(2,1)}, u32[]{:S(2)}, u32[]{:S(2)}) async-start(bf16[32,128,256]{2,1,0:T(8,128)(2,1)} %bitcast.56), calls=%async_computation.1 | async-start | bytes 4194304 | tf_op jit(solution)/shard_map/all_to_all | solution.py:79
  97.5 3.5 %fusion.28 = f32[512,256,1]{1,0,2:T(8,128)S(1)} fusion(bf16[32,128,512]{2,1,0:T(8,128)(2,1)} %copy-done.1, bf16[32,128,256]{2,1,0:T(8,128)(2,1)S(1)} %all-to-all-done.4), kind=kOutput, calls=%fused_computation.40 | convolution fusion | flops 1073741824 | bytes 6815744 | tf_op jit(solution)/shard_map/dot_general | solution.py:96
  101.0 14.7 %fusion.20 = f32[32]{0:T(128)S(1)} fusion(bf16[32,512,256]{2,1,0:T(8,128)(2,1)} %param.16, f32[512,256,1]{1,0,2:T(8,128)S(1)} %fusion.28), kind=kOutput, calls=%fused_computation.22 | convolution fusion | flops 50331648 | bytes 8913024 | tf_op jit(solution)/shard_map/dot_general | solution.py:111
  115.7 31.3 %all-to-all-done.1 = bf16[32,128,256]{2,1,0:T(8,128)(2,1)} async-done(((bf16[32,128,256]{2,1,0:T(8,128)(2,1)}), bf16[32,128,256]{2,1,0:T(8,128)(2,1)}, u32[]{:S(2)}, u32[]{:S(2)}) %all-to-all-start.1) | async-done | bytes 2097184 | tf_op jit(solution)/shard_map/all_to_all | solution.py:79
  147.0 0.6 broadcast_in_dim.19
  147.6 6.1 %all-to-all-start.5 = ((f32[32,1,32]{2,1,0:T(1,128)}), f32[32,1,32]{2,1,0:T(1,128)S(1)}, u32[]{:S(2)}, u32[]{:S(2)}) async-start(f32[32,1,32]{2,1,0:T(1,128)} %broadcast_in_dim.19), calls=%async_computation.5 | async-start | bytes 32768 | tf_op jit(solution)/shard_map/all_to_all | solution.py:11
  153.7 0.0 copy-start.6
  153.7 0.0 copy-start.3
  153.7 5.0 %fusion.1 = f32[8,128,256]{2,1,0:T(8,128)} fusion(bf16[4096,256,1]{1,0,2:T(8,128)(2,1)} %bitcast.15, s32[4096]{0:T(1024)S(1)} %bitcast.63, s32[8,128]{1,0:T(8,128)S(1)} %multiply_add_fusion), kind=kOutput, calls=%fused_computation.3 | convolution fusion | flops 2151677952 | bytes 3166208 | tf_op jit(solution)/shard_map/dot_general | solution.py:85
  158.7 4.7 %all-to-all-done.5 = f32[32,1,32]{2,1,0:T(1,128)S(1)} async-done(((f32[32,1,32]{2,1,0:T(1,128)}), f32[32,1,32]{2,1,0:T(1,128)S(1)}, u32[]{:S(2)}, u32[]{:S(2)}) %all-to-all-start.5) | async-done | bytes 4128 | tf_op jit(solution)/shard_map/all_to_all | solution.py:11
  163.4 5.6 %all-to-all-start.2 = ((f32[8,128,256]{2,1,0:T(8,128)}), f32[8,128,256]{2,1,0:T(8,128)S(1)}, u32[]{:S(2)}, u32[]{:S(2)}) async-start(f32[8,128,256]{2,1,0:T(8,128)} %fusion.1), calls=%async_computation.2 | async-start | bytes 2097152 | tf_op jit(solution)/shard_map/all_to_all | solution.py:33
  169.0 0.2 reduce-window.8
  169.2 0.1 convert_reduce_fusion
  169.3 0.5 reduce_sum.29
  169.8 13.0 %all-to-all-done.2 = f32[8,128,256]{2,1,0:T(8,128)S(1)} async-done(((f32[8,128,256]{2,1,0:T(8,128)}), f32[8,128,256]{2,1,0:T(8,128)S(1)}, u32[]{:S(2)}, u32[]{:S(2)}) %all-to-all-start.2) | async-done | bytes 1048608 | tf_op jit(solution)/shard_map/all_to_all | solution.py:33
  182.9 0.1 reduce_sum.27
  182.9 0.0 copy-done.3
  182.9 0.9 fusion.19
  (13 shorter events, 0.1 us)
Async XLA Ops:
  0.6 42.0 %copy-start = (bf16[1024,512]{1,0:T(8,128)(2,1)S(1)}, bf16[1024,512]{1,0:T(8,128)(2,1)}, u32[]{:S(2)}) copy-start(bf16[1024,512]{1,0:T(8,128)(2,1)} %param.10) | copy-start | bytes 3145732
  38.5 4.0 %copy-start.2 = (s32[1,32,128]{2,1,0:T(8,128)S(1)}, s32[1,32,128]{2,1,0:T(8,128)}, u32[]{:S(2)}) copy-start(s32[1,32,128]{2,1,0:T(8,128)} %param.12) | copy-start | bytes 49156
  38.5 54.3 %all-to-all-start.4 = ((bf16[32,128,256]{2,1,0:T(8,128)(2,1)}), bf16[32,128,256]{2,1,0:T(8,128)(2,1)S(1)}, u32[]{:S(2)}, u32[]{:S(2)}) async-start(bf16[32,128,256]{2,1,0:T(8,128)(2,1)} %bitcast.55), calls=%async_computation.4 | async-start | bytes 4194304 | tf_op jit(solution)/shard_map/all_to_all | solution.py:89
  42.6 17.3 %copy-start.4 = (s32[1,32]{1,0:T(1,128)S(1)}, s32[1,32]{1,0:T(1,128)}, u32[]{:S(2)}) copy-start(s32[1,32]{1,0:T(1,128)} %param.14) | copy-start | bytes 388
  59.9 3.9 %copy-start.5 = (f32[1,32]{1,0:T(1,128)S(1)}, f32[1,32]{1,0:T(1,128)}, u32[]{:S(2)}) copy-start(f32[1,32]{1,0:T(1,128)} %param.15) | copy-start | bytes 388
  63.8 13.0 %copy-start.1 = (bf16[32,128,512]{2,1,0:T(8,128)(2,1)}, bf16[32,128,512]{2,1,0:T(8,128)(2,1)S(1)}, u32[]{:S(2)}) copy-start(bf16[32,128,512]{2,1,0:T(8,128)(2,1)S(1)} %fusion.15) | copy-start | bytes 12582916
  92.8 54.1 %all-to-all-start.1 = ((bf16[32,128,256]{2,1,0:T(8,128)(2,1)}), bf16[32,128,256]{2,1,0:T(8,128)(2,1)}, u32[]{:S(2)}, u32[]{:S(2)}) async-start(bf16[32,128,256]{2,1,0:T(8,128)(2,1)} %bitcast.56), calls=%async_computation.1 | async-start | bytes 4194304 | tf_op jit(solution)/shard_map/all_to_all | solution.py:79
  147.6 15.9 %all-to-all-start.5 = ((f32[32,1,32]{2,1,0:T(1,128)}), f32[32,1,32]{2,1,0:T(1,128)S(1)}, u32[]{:S(2)}, u32[]{:S(2)}) async-start(f32[32,1,32]{2,1,0:T(1,128)} %broadcast_in_dim.19), calls=%async_computation.5 | async-start | bytes 32768 | tf_op jit(solution)/shard_map/all_to_all | solution.py:11
  153.7 15.3 %copy-start.6 = (s32[4]{0:T(128)S(1)}, s32[4]{0:T(128)}, u32[]{:S(2)}) copy-start(s32[4]{0:T(128)} %param.18) | copy-start | bytes 52
  153.7 29.2 %copy-start.3 = (f32[4,256]{1,0:T(4,128)S(1)}, f32[4,256]{1,0:T(4,128)}, u32[]{:S(2)}) copy-start(f32[4,256]{1,0:T(4,128)} %param.17) | copy-start | bytes 12292
  163.4 19.4 %all-to-all-start.2 = ((f32[8,128,256]{2,1,0:T(8,128)}), f32[8,128,256]{2,1,0:T(8,128)S(1)}, u32[]{:S(2)}, u32[]{:S(2)}) async-start(f32[8,128,256]{2,1,0:T(8,128)} %fusion.1), calls=%async_computation.2 | async-start | bytes 2097152 | tf_op jit(solution)/shard_map/all_to_all | solution.py:33
where the time goes:
time: 187 us; the launch traced here: 184 us
  waiting for transfers between devices  62.5 us (33%)
  matrix products  49.3 us (26%)
  blocking collectives  31.2 us (17%)
  starting transfers between devices  20.4 us (11%)
  local copies, waits for them, and re-layouts  18.8 us (10%)
    all_to_all x1, waiting for transfers between devices, on_device(): lax.all_to_all(outgoing, 'dst', split_axis=0, concat_axis=0, tiled=True)  31.3 us
    all_to_all x1, blocking collectives, on_device(): lax.all_to_all(slot_local, 'dst', split_axis=0, concat_axis=0, tiled=True)  18.3 us
    gather x1, local copies, waits for them, and re-layouts, on_device(): jnp.take(node_table, src_ids[0].reshape(-1), axis=0)  17.3 us
    dot_general x1, matrix products, on_device(): jnp.dot(basis_flat, outer_sum.reshape(-1), precision=highest)  14.7 us
    all_to_all x1, waiting for transfers between devices, on_device(): lax.all_to_all(wanted.reshape(block_count, block_rows, out_cols), 'dst',...  13.4 us
    all_to_all x1, waiting for transfers between devices, summed_on_arrival(): tiles = lax.all_to_all(cut_along(x, dim, devices), axis, 0, 0, tiled=True)  13 us
    dot_general x1, matrix products, on_device(): mixing = jnp.dot(basis_coef[0], basis_flat, precision=highest)  13 us
    all_to_all x1, blocking collectives, copy_for_each(): lax.all_to_all(jnp.broadcast_to(x[None], (devices, *x.shape)), axis, 0, 0...  12.9 us
  transfers between devices with their start and end apart: 4, of which 4 were waited for; matrix products, arithmetic and copies ran while one was open for 33% of the time, Pallas kernels for 0%

commit v1 on v0

v1 whole, which is shorter than its diff:
```python
import jax
import jax.numpy as jnp
from jax import lax
from jax.experimental import pallas as pl
from jax.experimental.pallas import tpu as pltpu
from jax.sharding import PartitionSpec as P

MESH = pl.DeviceIdType.MESH
BF = jnp.bfloat16
F32 = jnp.float32
NX, NC, NZ, NY, NM = 4, 2, 8, 2, 2
NR, ND = NX * NC, NZ * NY
TAB, F, H, BLK, ROWS, BASES = 1024, 512, 256, 128, 128, 32
OWN = NR * ROWS
CHUNK = 2 * BLK


def offset(k):
    step = k // 2
    far = (step // 2 + 1) * (1 - 2 * (step % 2)) * (1 - step // (NZ - 1))
    return far, k % 2


def kernel(
    table, edge, src_ids, dst_ids, mask, coef, basis, bias, type_rows, cot,
    out, grad,
    tbl, edg, sid, bas, hot, sbuf, rbuf, ids, hot_t, acc, accb, gbuf, wall, wbuf,
    s_send, s_recv, s_all, z_sib, z_sibr, z_own, z_send, z_recv, part, p_send, p_recv,
    load_sem, c_ss, c_rs, i_ss, i_rs, g_ss, g_rs, w_sem, s_sem, sib_sem, z_ss, z_rs, p_ss, p_rs,
):
    rel, dst, mp = lax.axis_index("rel"), lax.axis_index("dst"), lax.axis_index("mp")
    x, core = rel // NC, rel % NC
    z, y = dst // NY, dst % NY
    other = 1 - mp

    def load(i, src, to):
        return pltpu.make_async_copy(src, to, load_sem.at[i])

    loads = [
        load(0, table.at[:, pl.ds(pl.multiple_of(mp * H, H), H)], tbl),
        load(1, edge, edg),
        load(2, src_ids, sid),
        load(3, cot, gbuf.at[mp, pl.ds(pl.multiple_of(rel * ROWS, ROWS), ROWS)]),
        load(4, dst_ids.at[dst], ids.at[dst]),
        load(5, basis, bas),
    ]
    for copy in loads:
        copy.start()

    barrier = pltpu.get_barrier_semaphore()

    def greet_dst(q, _):
        to = {"dst": (dst + q // NM) % ND, "mp": (mp + q % NM) % NM}
        pl.semaphore_signal(barrier, inc=1, device_id=to, device_id_type=MESH)
        return 0

    def greet_rel(q, _):
        to = {"rel": (rel + q // NM) % NR, "mp": (mp + q % NM) % NM}
        pl.semaphore_signal(barrier, inc=1, device_id=to, device_id_type=MESH)
        return 0

    lax.fori_loop(1, ND * NM, greet_dst, 0)
    lax.fori_loop(NM, NR * NM, greet_rel, 0)

    lanes = lax.broadcasted_iota(jnp.int32, (BLK, BLK), 1)

    def make_chunk(d, to):
        for half in range(2):
            k = 2 * d + half
            row = sid[pl.ds(k, 1), :]
            col = jnp.broadcast_to(row, (BLK, BLK)).T
            for t in range(TAB // BLK):
                hot[half * BLK : (half + 1) * BLK, t * BLK : (t + 1) * BLK] = jnp.where(
                    lanes + t * BLK == col, 1.0, 0.0
                ).astype(BF)
        picked = jnp.dot(hot[...], tbl[...], preferred_element_type=F32).astype(BF)
        for half in range(2):
            k = 2 * d + half
            live = mask[0, k].astype(F32)
            block = (edg[k].astype(F32) * live).astype(BF)
            to[half * BLK : (half + 1) * BLK, :] = jnp.dot(
                block, picked[half * BLK : (half + 1) * BLK, :], preferred_element_type=F32
            ).astype(BF)

    for i in (0, 1, 2):
        loads[i].wait()
    make_chunk(dst, rbuf.at[dst])
    loads[3].wait()
    loads[4].wait()
    pl.semaphore_wait(barrier, ND * NM - 1 + NR * NM - NM)

    def peer(k, sign):
        dz, dy = offset(k)
        return ((z + sign * dz + NZ) % NZ) * NY + (y + dy) % NY

    def kth(i):
        return i + i // (ND - 2)

    def id_copy(k):
        to = peer(k, 1)
        return pltpu.make_async_remote_copy(
            dst_ids.at[to], ids.at[dst], i_ss.at[to], i_rs.at[dst],
            device_id={"dst": to}, device_id_type=MESH)

    def chunk_copy(k):
        to = peer(k, 1)
        return pltpu.make_async_remote_copy(
            sbuf.at[to], rbuf.at[dst], c_ss.at[to], c_rs.at[dst],
            device_id={"dst": to}, device_id_type=MESH)

    def grad_copy(q):
        to_r, to_m = (rel + q // NM) % NR, (mp + q % NM) % NM
        mine = gbuf.at[mp, pl.ds(pl.multiple_of(rel * ROWS, ROWS), ROWS)]
        slot = rel * NM + mp
        return pltpu.make_async_remote_copy(
            mine, mine, g_ss.at[to_r * NM + to_m], g_rs.at[slot],
            device_id={"rel": to_r, "mp": to_m}, device_id_type=MESH)

    def send_ids(i, _):
        id_copy(kth(i)).start()
        return 0

    lax.fori_loop(0, ND - 1, send_ids, 0)

    def send_chunk(i, _):
        k = kth(i)
        to = peer(k, 1)
        make_chunk(to, sbuf.at[to])
        chunk_copy(k).start()
        return 0

    lax.fori_loop(0, ND - 1, send_chunk, 0)

    def send_grad(q, _):
        grad_copy(q).start()
        return 0

    lax.fori_loop(1, NR * NM, send_grad, 0)

    loads[5].wait()
    TILE = 32

    def mix(t, _):
        at = pl.multiple_of(t * TILE, TILE)
        total = coef[0, 0] * bas[0, pl.ds(at, TILE), :].astype(F32)
        for b in range(1, BASES):
            total = total + coef[0, b] * bas[b, pl.ds(at, TILE), :].astype(F32)
        wall[pl.ds(at, TILE), :] = total.astype(BF)
        return 0

    lax.fori_loop(0, F // TILE, mix, 0)
    w_copy = pltpu.make_async_remote_copy(
        wall.at[pl.ds(pl.multiple_of(other * H, H), H)], wbuf.at[mp], w_sem.at[0], w_sem.at[1],
        device_id={"mp": other}, device_id_type=MESH)
    w_copy.start()
    wbuf[mp] = wall[pl.ds(pl.multiple_of(mp * H, H), H), :]

    rows = lax.broadcasted_iota(jnp.int32, (OWN, BLK), 0)

    def add_chunk(s):
        for half in range(2):
            row = ids[s, half : half + 1, :]
            hot_t[:, half * BLK : (half + 1) * BLK] = jnp.where(rows == row, 1.0, 0.0).astype(BF)
        acc[...] += jnp.dot(hot_t[...], rbuf[s], preferred_element_type=F32)

    acc[...] = jnp.zeros_like(acc)
    add_chunk(dst)

    def take_chunk(i, _):
        s = peer(kth(i), -1)
        pltpu.make_async_remote_copy(
            dst_ids.at[s], ids.at[s], i_ss.at[s], i_rs.at[s],
            device_id={"dst": s}, device_id_type=MESH).wait_recv()
        pltpu.make_async_remote_copy(
            sbuf.at[s], rbuf.at[s], c_ss.at[s], c_rs.at[s],
            device_id={"dst": s}, device_id_type=MESH).wait_recv()
        add_chunk(s)
        return 0

    lax.fori_loop(0, ND - 1, take_chunk, 0)

    def take_grad(q, _):
        fr, fm = (rel + q // NM) % NR, (mp + q % NM) % NM
        theirs = gbuf.at[fm, pl.ds(pl.multiple_of(fr * ROWS, ROWS), ROWS)]
        slot = fr * NM + fm
        pltpu.make_async_remote_copy(
            theirs, theirs, g_ss.at[slot], g_rs.at[slot],
            device_id={"rel": fr, "mp": fm}, device_id_type=MESH).wait_recv()
        return 0

    lax.fori_loop(1, NR * NM, take_grad, 0)
    w_copy.wait_recv()

    accb[...] = acc[...].astype(BF)
    contract = (((0,), (0,)), ((), ()))

    def outer(g):
        return lax.dot_general(accb[...], gbuf[g], contract, preferred_element_type=F32)

    s_send[...] = outer(other).astype(BF)
    s_copy = pltpu.make_async_remote_copy(
        s_send, s_recv, s_sem.at[0], s_sem.at[1], device_id={"mp": other}, device_id_type=MESH)
    s_copy.start()

    def times_w(at, g):
        return jnp.dot(accb[pl.ds(pl.multiple_of(at, ROWS), ROWS), :], wbuf[g], preferred_element_type=F32)

    for xx in range(NX):
        for g in range(NM):
            z_sib[xx, g] = times_w((xx * NC + 1 - core) * ROWS, g).astype(BF)
    sib_copy = pltpu.make_async_remote_copy(
        z_sib, z_sibr, sib_sem.at[0], sib_sem.at[1],
        device_id={"rel": x * NC + 1 - core}, device_id_type=MESH)
    sib_copy.start()
    for xx in range(NX):
        for g in range(NM):
            z_own[xx, g] = times_w((xx * NC + core) * ROWS, g)
    s_all[pl.ds(pl.multiple_of(mp * H, H), H), :] = outer(mp)

    sib_copy.wait_recv()

    def z_copy(q):
        tx, tm = (x + q // NM) % NX, (mp + q % NM) % NM
        return pltpu.make_async_remote_copy(
            z_send.at[tx, tm], z_recv.at[x * NM + mp], z_ss.at[tx * NM + tm], z_rs.at[x * NM + mp],
            device_id={"rel": tx * NC + core, "mp": tm}, device_id_type=MESH)

    for q in range(1, NX * NM):
        tx, tm = (x + q // NM) % NX, (mp + q % NM) % NM
        z_send[tx, tm] = (z_own[tx, tm] + z_sibr[tx, tm].astype(F32)).astype(BF)
        z_copy(q).start()
    z_recv[x * NM + mp] = (z_own[x, mp] + z_sibr[x, mp].astype(F32)).astype(BF)

    DT = 16

    def against(base):
        def step(t, sums):
            at = pl.multiple_of(base + t * DT, DT)
            s = s_all[pl.ds(at, DT), :]
            new = []
            for b in range(BASES):
                v = bas[b, pl.ds(at, DT), :].astype(F32) * s
                v = (v[0:8, 0:128] + v[8:16, 0:128]) + (v[0:8, 128:256] + v[8:16, 128:256])
                new.append(sums[b] + v)
            return tuple(new)
        return step

    zeros = tuple(jnp.zeros((8, 128), F32) for _ in range(BASES))
    sums = lax.fori_loop(0, H // DT, against(mp * H), zeros)
    s_copy.wait_recv()
    s_all[pl.ds(pl.multiple_of(other * H, H), H), :] = s_recv[...].astype(F32)
    sums = lax.fori_loop(0, H // DT, against(other * H), sums)
    for b in range(BASES):
        part[b : b + 1, :] = jnp.sum(sums[b], axis=0, keepdims=True)
    mine = jnp.sum(part[...].T, axis=0, keepdims=True)
    me = dst * NM + mp
    p_send[...] = mine
    p_recv[me] = mine

    def part_copy(q):
        td, tm = (dst + q // NM) % ND, (mp + q % NM) % NM
        return pltpu.make_async_remote_copy(
            p_send, p_recv.at[me], p_ss.at[td * NM + tm], p_rs.at[me],
            device_id={"dst": td, "mp": tm}, device_id_type=MESH)

    def send_part(q, _):
        part_copy(q).start()
        return 0

    lax.fori_loop(1, ND * NM, send_part, 0)

    for q in range(1, NX * NM):
        fx, fm = (x + q // NM) % NX, (mp + q % NM) % NM
        slot = fx * NM + fm
        pltpu.make_async_remote_copy(
            z_send.at[fx, fm], z_recv.at[slot], z_ss.at[slot], z_rs.at[slot],
            device_id={"rel": fx * NC + core, "mp": fm}, device_id_type=MESH).wait_recv()
    total = z_recv[0].astype(F32)
    for q in range(1, NX * NM):
        total = total + z_recv[q].astype(F32)
    at = lax.broadcasted_iota(jnp.int32, (ROWS, H), 0) + rel * ROWS
    bound = type_rows[0]
    row_bias = jnp.broadcast_to(bias[0:1, :], (ROWS, H))
    for c in range(1, 4):
        row_bias = jnp.where(at >= bound, bias[c : c + 1, :], row_bias)
        bound = bound + type_rows[c]
    out[...] = (total + row_bias).astype(BF)

    def take_part(q, _):
        fd, fm = (dst + q // NM) % ND, (mp + q % NM) % NM
        slot = fd * NM + fm
        pltpu.make_async_remote_copy(
            p_send, p_recv.at[slot], p_ss.at[slot], p_rs.at[slot],
            device_id={"dst": fd, "mp": fm}, device_id_type=MESH).wait_recv()
        return 0

    lax.fori_loop(1, ND * NM, take_part, 0)
    total = p_recv[0]
    for q in range(1, ND * NM):
        total = total + p_recv[q]
    grad[...] = total

    def done_ids(i, _):
        id_copy(kth(i)).wait_send()
        chunk_copy(kth(i)).wait_send()
        return 0

    def done_grad(q, _):
        grad_copy(q).wait_send()
        return 0

    def done_part(q, _):
        part_copy(q).wait_send()
        return 0

    lax.fori_loop(0, ND - 1, done_ids, 0)
    lax.fori_loop(1, NR * NM, done_grad, 0)
    lax.fori_loop(1, ND * NM, done_part, 0)
    w_copy.wait_send()
    s_copy.wait_send()
    sib_copy.wait_send()
    for q in range(1, NX * NM):
        z_copy(q).wait_send()


def on_device(
    node_table, edge_weights, src_ids, dst_ids, block_mask,
    basis_coef, basis_mats, type_bias, type_rows, cotangent,
):
    anywhere = pl.BlockSpec(memory_space=pl.ANY)
    vmem = pl.BlockSpec(memory_space=pltpu.VMEM)
    smem = pl.BlockSpec(memory_space=pltpu.SMEM)
    dma = pltpu.SemaphoreType.DMA
    return pl.pallas_call(
        kernel,
        out_shape=(
            jax.ShapeDtypeStruct((ROWS, H), BF),
            jax.ShapeDtypeStruct((1, BASES), F32),
        ),
        in_specs=[anywhere, anywhere, anywhere, anywhere, smem, smem, anywhere, vmem, smem, anywhere],
        out_specs=(vmem, vmem),
        scratch_shapes=[
            pltpu.VMEM((TAB, H), BF),
            pltpu.VMEM((2 * ND, BLK, BLK), BF),
            pltpu.VMEM((2 * ND, BLK), jnp.int32),
            pltpu.VMEM((BASES, F, H), BF),
            pltpu.VMEM((CHUNK, TAB), BF),
            pltpu.VMEM((ND, CHUNK, H), BF),
            pltpu.VMEM((ND, CHUNK, H), BF),
            pltpu.VMEM((ND, 2, BLK), jnp.int32),
            pltpu.VMEM((OWN, CHUNK), BF),
            pltpu.VMEM((OWN, H), F32),
            pltpu.VMEM((OWN, H), BF),
            pltpu.VMEM((NM, OWN, H), BF),
            pltpu.VMEM((F, H), BF),
            pltpu.VMEM((NM, H, H), BF),
            pltpu.VMEM((H, H), BF),
            pltpu.VMEM((H, H), BF),
            pltpu.VMEM((F, H), F32),
            pltpu.VMEM((NX, NM, ROWS, H), BF),
            pltpu.VMEM((NX, NM, ROWS, H), BF),
            pltpu.VMEM((NX, NM, ROWS, H), F32),
            pltpu.VMEM((NX, NM, ROWS, H), BF),
            pltpu.VMEM((NX * NM, ROWS, H), BF),
            pltpu.VMEM((BASES, 128), F32),
            pltpu.VMEM((1, BASES), F32),
            pltpu.VMEM((ND * NM, 1, BASES), F32),
            dma((6,)),
            dma((ND,)), dma((ND,)), dma((ND,)), dma((ND,)),
            dma((NR * NM,)), dma((NR * NM,)),
            dma((2,)), dma((2,)), dma((2,)),
            dma((NX * NM,)), dma((NX * NM,)),
            dma((ND * NM,)), dma((ND * NM,)),
        ],
        compiler_params=pltpu.CompilerParams(
            collective_id=0, has_side_effects=True, vmem_limit_bytes=50 * 1024 * 1024
        ),
        name="relational_layer",
    )(
        node_table, edge_weights[0], src_ids[0], dst_ids[0].reshape(ND, 2, BLK), block_mask,
        basis_coef, basis_mats, type_bias, type_rows, cotangent,
    )


def solution(mesh):
    in_specs = (
        P(("rel", "dst"), None),
        P("rel", "dst", None, None),
        P("rel", "dst", None),
        P("rel", "dst", None),
        P("rel", "dst"),
        P("rel", None),
        P(None, None, "mp"),
        P(None, "mp"),
        P(),
        P(("rel", "dst"), "mp"),
    )
    out_specs = (P(("rel", "dst"), "mp"), P("rel", None))
    return jax.shard_map(
        on_device, mesh=mesh, in_specs=in_specs, out_specs=out_specs, check_vma=False
    )
```

time: 187 us -> 95 us (0.51)
  the two profiles are of different devices: /device:TPU:6 before, /device:TPU:2 now
where the time goes in v1:
time: 95 us; the launch traced here: 94.6 us
  Pallas kernels  85.5 us (90%)
  local copies, waits for them, and re-layouts  8.51 us (9%)
    pallas_call x1, Pallas kernels, on_device(): pl.pallas_call(kernel, out_shape=(jax.ShapeDtypeStruct((ROWS, H), BF), ja...  85.5 us
    unnamed x20, local copies, waits for them, and re-layouts  8.51 us

profile of v1, /device:TPU:2, one launch (start us, length us, event | category | flops | bytes accessed | tf_op | source)
XLA Modules:
  0.0 94.6 jit_solution(6263974698760989087)
XLA Ops:
  0.6 0.0 copy-start
  0.6 1.2 %copy-done = bf16[1024,512]{1,0:T(8,128)(2,1)S(1)} copy-done((bf16[1024,512]{1,0:T(8,128)(2,1)S(1)}, bf16[1024,512]{1,0:T(8,128)(2,1)}, u32[]{:S(2)}) %copy-start) | copy-done | bytes 1048600
  1.9 0.0 copy-start.1
  1.9 1.2 %copy-done.1 = bf16[1,32,128,128]{3,2,1,0:T(8,128)(2,1)S(1)} copy-done((bf16[1,32,128,128]{3,2,1,0:T(8,128)(2,1)S(1)}, bf16[1,32,128,128]{3,2,1,0:T(8,128)(2,1)}, u32[]{:S(2)}) %copy-start.1) | copy-done | bytes 1048600
  3.1 0.0 copy-start.2
  3.1 0.8 copy-done.2
  3.9 0.0 copy-start.3
  3.9 0.7 copy-done.3
  4.6 0.0 copy-start.4
  4.6 0.7 copy-done.4
  5.4 0.0 copy-start.5
  5.4 0.7 copy-done.5
  6.0 0.0 copy-start.6
  6.0 0.7 copy-done.6
  6.7 0.0 copy-start.7
  6.7 0.7 copy-done.7
  7.4 0.0 copy-start.8
  7.4 0.7 copy-done.8
  8.0 85.5 %relational_layer.1 = (bf16[128,256]{1,0:T(8,128)(2,1)S(1)}, f32[1,32]{1,0:T(1,128)S(1)}) custom-call(bf16[1024,512]{1,0:T(8,128)(2,1)S(1)} %copy-done, bf16[32,128,128]{2,1,0:T(8,128)(2,1)S(1)} %bitcast.3, s32[32,128]{1,0:T(8,128)S(1)} %bitcast.4, s32[16,2,128]{2,1,0:T(2,128)S(1)} %bitcast.5, s32[1,32]{1,0:T(1,128)S(1)} %copy-done.6, ...), custom_call_target="tpu_custom_call" | custom-call | tf_op jit(solution)/shard_map/relational_layer/pallas_call | solution.py:334
  93.5 0.6 copy.14
  94.1 0.5 copy.15
Async XLA Ops:
  0.6 1.2 %copy-start = (bf16[1024,512]{1,0:T(8,128)(2,1)S(1)}, bf16[1024,512]{1,0:T(8,128)(2,1)}, u32[]{:S(2)}) copy-start(bf16[1024,512]{1,0:T(8,128)(2,1)} %table.1) | copy-start | bytes 3145732
  1.9 1.2 %copy-start.1 = (bf16[1,32,128,128]{3,2,1,0:T(8,128)(2,1)S(1)}, bf16[1,32,128,128]{3,2,1,0:T(8,128)(2,1)}, u32[]{:S(2)}) copy-start(bf16[1,32,128,128]{3,2,1,0:T(8,128)(2,1)} %param.11) | copy-start | bytes 3145732
  3.1 0.8 copy-start.2
  3.9 0.7 copy-start.3
  4.6 0.7 copy-start.4
  5.4 0.7 copy-start.5
  6.0 0.7 copy-start.6
  6.7 0.7 copy-start.7
  7.4 0.7 copy-start.8

commit v2 on v1

v2 whole, which is shorter than its diff:
```python
import jax
import jax.numpy as jnp
from jax import lax
from jax.experimental import pallas as pl
from jax.experimental.pallas import tpu as pltpu
from jax.sharding import PartitionSpec as P

MESH = pl.DeviceIdType.MESH
BF = jnp.bfloat16
F32 = jnp.float32
NX, NC, NZ, NY, NM = 4, 2, 8, 2, 2
NR, ND = NX * NC, NZ * NY
TAB, F, H, BLK, ROWS, BASES = 1024, 512, 256, 128, 128, 32
OWN = NR * ROWS
CHUNK = 2 * BLK
EARLY = 6


def offset(k):
    step = k // 2
    far = (step // 2 + 1) * (1 - 2 * (step % 2)) * (1 - step // (NZ - 1))
    return far, k % 2


def kernel(
    table, edge, src_ids, dst_ids, mask_any, coef_any, basis, bias_any, rows_any, cot,
    out, grad,
    mask, coef, type_rows, bias,
    tbl, edg, sid, bas, hot, sbuf, rbuf, ids, hot_t, acc, accb, acct, gbuf, wall, wbuf,
    s_send, s_recv, s_all, z_sib, z_sibr, z_own, z_send, z_recv, part, p_send, p_recv,
    load_sem, c_ss, c_rs, i_ss, i_rs, g_ss, g_rs, w_sem, s_sem, sib_ss, sib_rs, z_ss, z_rs, p_ss, p_rs,
):
    rel, dst, mp = lax.axis_index("rel"), lax.axis_index("dst"), lax.axis_index("mp")
    x, core = rel // NC, rel % NC
    z, y = dst // NY, dst % NY
    other = 1 - mp

    def load(i, src, to):
        return pltpu.make_async_copy(src, to, load_sem.at[i])

    def remote(src, to, ss, rs, **where):
        return pltpu.make_async_remote_copy(src, to, ss, rs, device_id=where, device_id_type=MESH)

    loads = [
        load(0, src_ids, sid),
        load(1, mask_any, mask),
        load(2, table.at[:, pl.ds(pl.multiple_of(mp * H, H), H)], tbl),
        load(3, edge, edg),
        load(4, dst_ids.at[dst], ids.at[dst]),
        load(5, cot, gbuf.at[core, mp, x]),
        load(6, coef_any, coef),
        load(7, rows_any, type_rows),
        load(8, bias_any, bias),
        load(9, basis, bas),
    ]
    for copy in loads[:9]:
        copy.start()

    barrier = pltpu.get_barrier_semaphore()
    group = [q for q in range(1, ND * NM)]
    across = [(dx, dm) for dx in range(1, NX) for dm in range(NM)]

    def greet(**where):
        pl.semaphore_signal(barrier, inc=1, device_id=where, device_id_type=MESH)

    for q in group:
        greet(dst=(dst + q // NM) % ND, mp=(mp + q % NM) % NM)
    for dx, dm in across:
        greet(rel=(x + dx) % NX * NC + core, mp=(mp + dm) % NM)
    sibling = x * NC + 1 - core
    greet(rel=sibling)

    lanes = lax.broadcasted_iota(jnp.int32, (BLK, BLK), 1)

    def make_chunk(d, to):
        for half in range(2):
            k = 2 * d + half
            row = sid[pl.ds(k, 1), :]
            col = jnp.broadcast_to(row, (BLK, BLK)).T
            for t in range(TAB // BLK):
                hot[half * BLK : (half + 1) * BLK, t * BLK : (t + 1) * BLK] = jnp.where(
                    lanes + t * BLK == col, 1.0, 0.0
                ).astype(BF)
        picked = jnp.dot(hot[...], tbl[...], preferred_element_type=F32).astype(BF)
        for half in range(2):
            k = 2 * d + half
            live = mask[0, k].astype(F32)
            block = (edg[k].astype(F32) * live).astype(BF)
            to[half * BLK : (half + 1) * BLK, :] = jnp.dot(
                block, picked[half * BLK : (half + 1) * BLK, :], preferred_element_type=F32
            ).astype(BF)

    def peer(k, sign):
        dz, dy = offset(k)
        return ((z + sign * dz + NZ) % NZ) * NY + (y + dy) % NY

    def kth(i):
        return i + i // (ND - 2)

    def id_copy(to):
        return remote(dst_ids.at[to], ids.at[dst], i_ss.at[to], i_rs.at[dst], dst=to)

    def chunk_copy(to):
        return remote(sbuf.at[to], rbuf.at[dst], c_ss.at[to], c_rs.at[dst], dst=to)

    def make(i, _):
        to = peer(kth(i), 1)
        make_chunk(to, sbuf.at[to])
        return 0

    def send(i, _):
        chunk_copy(peer(kth(i), 1)).start()
        return 0

    def send_ids(i, _):
        id_copy(peer(kth(i), 1)).start()
        return 0

    def make_send(i, _):
        make(i, 0)
        return send(i, 0)

    for i in range(4):
        loads[i].wait()
    lax.fori_loop(0, EARLY, make, 0)
    loads[4].wait()
    loads[5].wait()
    pl.semaphore_wait(barrier, len(group) + len(across) + 1)
    lax.fori_loop(0, EARLY, send, 0)
    lax.fori_loop(0, ND - 1, send_ids, 0)
    mine = gbuf.at[core, mp, x]
    g_pair = remote(mine, mine, g_ss.at[0], g_rs.at[0], mp=other)
    g_pair.start()
    loads[9].start()
    lax.fori_loop(EARLY, ND - 1, make_send, 0)
    make_chunk(dst, rbuf.at[dst])

    g_pair.wait_recv()

    def g_across(dx):
        both = gbuf.at[core, :, x]
        return remote(both, both, g_ss.at[dx], g_rs.at[dx], rel=(x + dx) % NX * NC + core)

    for dx in range(1, NX):
        g_across(dx).start()

    for i in (6, 7, 8, 9):
        loads[i].wait()
    TILE = 32

    def mix(t, _):
        at = pl.multiple_of(t * TILE, TILE)
        total = coef[0, 0] * bas[0, pl.ds(at, TILE), :].astype(F32)
        for b in range(1, BASES):
            total = total + coef[0, b] * bas[b, pl.ds(at, TILE), :].astype(F32)
        wall[pl.ds(at, TILE), :] = total.astype(BF)
        return 0

    lax.fori_loop(0, F // TILE, mix, 0)
    w_copy = remote(wall.at[pl.ds(pl.multiple_of(other * H, H), H)], wbuf.at[mp], w_sem.at[0], w_sem.at[1], mp=other)
    w_copy.start()
    wbuf[mp] = wall[pl.ds(pl.multiple_of(mp * H, H), H), :]

    place = lax.broadcasted_iota(jnp.int32, (OWN, BLK), 0)
    half_rows = NX * ROWS
    rows = ((place % half_rows) // ROWS * NC + place // half_rows) * ROWS + place % ROWS

    def add_chunk(s):
        for half in range(2):
            row = ids[s, half : half + 1, :]
            hot_t[:, half * BLK : (half + 1) * BLK] = jnp.where(rows == row, 1.0, 0.0).astype(BF)
        return jnp.dot(hot_t[...], rbuf[s], preferred_element_type=F32)

    acc[...] = add_chunk(dst)

    def take(i):
        s = peer(kth(i), -1)
        remote(dst_ids.at[s], ids.at[s], i_ss.at[s], i_rs.at[s], dst=s).wait_recv()
        remote(sbuf.at[s], rbuf.at[s], c_ss.at[s], c_rs.at[s], dst=s).wait_recv()
        return add_chunk(s)

    def take_chunk(i, _):
        acc[...] += take(i)
        return 0

    lax.fori_loop(0, 8, take_chunk, 0)

    for dx in range(1, NX):
        theirs = gbuf.at[core, :, (x - dx + NX) % NX]
        remote(theirs, theirs, g_ss.at[dx], g_rs.at[dx], rel=(x - dx + NX) % NX * NC + core).wait_recv()
    g_sib = remote(gbuf.at[core], gbuf.at[core], g_ss.at[NX], g_rs.at[NX], rel=sibling)
    g_sib.start()

    lax.fori_loop(8, ND - 2, take_chunk, 0)
    g_sib.wait_recv()
    w_copy.wait_recv()

    accb[...] = (acc[...] + take(ND - 2)).astype(BF)
    acct[...] = accb[...].T

    def outer(g):
        return jnp.dot(acct[...], gbuf[:, g].reshape(OWN, H), preferred_element_type=F32)

    s_send[...] = outer(other).astype(BF)
    s_copy = remote(s_send, s_recv, s_sem.at[0], s_sem.at[1], mp=other)
    s_copy.start()

    def times_w(c, g):
        return jnp.dot(
            accb[pl.ds(pl.multiple_of(c * half_rows, half_rows), half_rows), :], wbuf[g],
            preferred_element_type=F32)

    def sib_copy(g):
        return remote(z_sib.at[g], z_sibr.at[g], sib_ss.at[g], sib_rs.at[g], rel=sibling)

    columns = (other, mp)
    for g in columns:
        z_sib[g] = times_w(1 - core, g).astype(BF)
        sib_copy(g).start()
    for g in columns:
        z_own[g] = times_w(core, g)

    def z_copy(dx, dm):
        tx, tm = (x + dx) % NX, (mp + dm) % NM
        return remote(
            z_send.at[tm, tx], z_recv.at[x * NM + mp], z_ss.at[tx * NM + tm], z_rs.at[x * NM + mp],
            rel=tx * NC + core, mp=tm)

    order = (2, 1, 3, 0)
    for dm in (1, 0):
        g = (mp + dm) % NM
        sib_copy(g).wait_recv()
        for dx in order:
            tx = (x + dx) % NX
            at = pl.ds(pl.multiple_of(tx * ROWS, ROWS), ROWS)
            piece = (z_own[g, at, :] + z_sibr[g, at, :].astype(F32)).astype(BF)
            if dx or dm:
                z_send[g, tx] = piece
                z_copy(dx, dm).start()
            else:
                z_recv[x * NM + mp] = piece

    s_all[pl.ds(pl.multiple_of(mp * H, H), H), :] = outer(mp)
    DT = 16

    def against(base):
        def step(t, sums):
            at = pl.multiple_of(base + t * DT, DT)
            s = s_all[pl.ds(at, DT), :]
            new = []
            for b in range(BASES):
                v = bas[b, pl.ds(at, DT), :].astype(F32) * s
                v = (v[0:8, 0:128] + v[8:16, 0:128]) + (v[0:8, 128:256] + v[8:16, 128:256])
                new.append(sums[b] + v)
            return tuple(new)
        return step

    zeros = tuple(jnp.zeros((8, 128), F32) for _ in range(BASES))
    sums = lax.fori_loop(0, H // DT, against(mp * H), zeros)

    def done_chunk(i, _):
        to = peer(kth(i), 1)
        id_copy(to).wait_send()
        chunk_copy(to).wait_send()
        return 0

    lax.fori_loop(0, ND - 1, done_chunk, 0)
    g_pair.wait_send()
    for dx in range(1, NX):
        g_across(dx).wait_send()
    g_sib.wait_send()
    w_copy.wait_send()

    s_copy.wait_recv()
    s_all[pl.ds(pl.multiple_of(other * H, H), H), :] = s_recv[...].astype(F32)
    sums = lax.fori_loop(0, H // DT, against(other * H), sums)
    for b in range(BASES):
        part[b : b + 1, :] = jnp.sum(sums[b], axis=0, keepdims=True)
    total = jnp.sum(part[...].T, axis=0, keepdims=True)
    me = dst * NM + mp
    p_send[...] = total
    p_recv[me] = total

    def part_copy(q):
        td, tm = (dst + q // NM) % ND, (mp + q % NM) % NM
        return remote(p_send, p_recv.at[me], p_ss.at[q], p_rs.at[q], dst=td, mp=tm)

    for q in group:
        part_copy(q).start()

    at = lax.broadcasted_iota(jnp.int32, (ROWS, H), 0) + rel * ROWS
    bound = type_rows[0]
    row_bias = jnp.broadcast_to(bias[0:1, :], (ROWS, H))
    for c in range(1, 4):
        row_bias = jnp.where(at >= bound, bias[c : c + 1, :], row_bias)
        bound = bound + type_rows[c]
    for dx, dm in across + [(0, 1)]:
        fx, fm = (x - dx + NX) % NX, (mp + dm) % NM
        slot = fx * NM + fm
        remote(
            z_send.at[fm, fx], z_recv.at[slot], z_ss.at[slot], z_rs.at[slot],
            rel=fx * NC + core, mp=fm).wait_recv()
    total = z_recv[0].astype(F32)
    for q in range(1, NX * NM):
        total = total + z_recv[q].astype(F32)
    out[...] = (total + row_bias).astype(BF)

    s_copy.wait_send()
    for dm in (1, 0):
        sib_copy((mp + dm) % NM).wait_send()
    for dx, dm in across + [(0, 1)]:
        z_copy(dx, dm).wait_send()
    for q in group:
        fd, fm = (dst - q // NM + ND) % ND, (mp + q % NM) % NM
        remote(p_send, p_recv.at[fd * NM + fm], p_ss.at[q], p_rs.at[q], dst=fd, mp=fm).wait_recv()
    total = p_recv[0]
    for q in range(1, ND * NM):
        total = total + p_recv[q]
    grad[...] = total
    for q in group:
        part_copy(q).wait_send()


def on_device(
    node_table, edge_weights, src_ids, dst_ids, block_mask,
    basis_coef, basis_mats, type_bias, type_rows, cotangent,
):
    anywhere = pl.BlockSpec(memory_space=pl.ANY)
    vmem = pl.BlockSpec(memory_space=pltpu.VMEM)
    dma = pltpu.SemaphoreType.DMA
    return pl.pallas_call(
        kernel,
        out_shape=(
            jax.ShapeDtypeStruct((ROWS, H), BF),
            jax.ShapeDtypeStruct((1, BASES), F32),
        ),
        in_specs=[anywhere] * 10,
        out_specs=(vmem, vmem),
        scratch_shapes=[
            pltpu.SMEM((1, 2 * ND), jnp.int32),
            pltpu.SMEM((1, BASES), F32),
            pltpu.SMEM((4,), jnp.int32),
            pltpu.VMEM((4, H), F32),
            pltpu.VMEM((TAB, H), BF),
            pltpu.VMEM((2 * ND, BLK, BLK), BF),
            pltpu.VMEM((2 * ND, BLK), jnp.int32),
            pltpu.VMEM((BASES, F, H), BF),
            pltpu.VMEM((CHUNK, TAB), BF),
            pltpu.VMEM((ND, CHUNK, H), BF),
            pltpu.VMEM((ND, CHUNK, H), BF),
            pltpu.VMEM((ND, 2, BLK), jnp.int32),
            pltpu.VMEM((OWN, CHUNK), BF),
            pltpu.VMEM((OWN, H), F32),
            pltpu.VMEM((OWN, H), BF),
            pltpu.VMEM((H, OWN), BF),
            pltpu.VMEM((NC, NM, NX, ROWS, H), BF),
            pltpu.VMEM((F, H), BF),
            pltpu.VMEM((NM, H, H), BF),
            pltpu.VMEM((H, H), BF),
            pltpu.VMEM((H, H), BF),
            pltpu.VMEM((F, H), F32),
            pltpu.VMEM((NM, NX * ROWS, H), BF),
            pltpu.VMEM((NM, NX * ROWS, H), BF),
            pltpu.VMEM((NM, NX * ROWS, H), F32),
            pltpu.VMEM((NM, NX, ROWS, H), BF),
            pltpu.VMEM((NX * NM, ROWS, H), BF),
            pltpu.VMEM((BASES, 128), F32),
            pltpu.VMEM((1, BASES), F32),
            pltpu.VMEM((ND * NM, 1, BASES), F32),
            dma((10,)),
            dma((ND,)), dma((ND,)), dma((ND,)), dma((ND,)),
            dma((NX + 1,)), dma((NX + 1,)),
            dma((2,)), dma((2,)), dma((NM,)), dma((NM,)),
            dma((NX * NM,)), dma((NX * NM,)),
            dma((ND * NM,)), dma((ND * NM,)),
        ],
        compiler_params=pltpu.CompilerParams(
            collective_id=0, has_side_effects=True, vmem_limit_bytes=67000000
        ),
        name="relational_layer",
    )(
        node_table, edge_weights[0], src_ids[0], dst_ids[0].reshape(ND, 2, BLK), block_mask,
        basis_coef, basis_mats, type_bias, type_rows, cotangent,
    )


def solution(mesh):
    in_specs = (
        P(("rel", "dst"), None),
        P("rel", "dst", None, None),
        P("rel", "dst", None),
        P("rel", "dst", None),
        P("rel", "dst"),
        P("rel", None),
        P(None, None, "mp"),
        P(None, "mp"),
        P(),
        P(("rel", "dst"), "mp"),
    )
    out_specs = (P(("rel", "dst"), "mp"), P("rel", None))
    return jax.shard_map(
        on_device, mesh=mesh, in_specs=in_specs, out_specs=out_specs, check_vma=False
    )
```

time: 95 us -> 82.2 us (0.87)
  the two profiles are of different devices: /device:TPU:2 before, /device:TPU:6 now
where the time goes in v2:
time: 82.2 us; the launch traced here: 82 us
  Pallas kernels  78.8 us (96%)
  local copies, waits for them, and re-layouts  2.59 us (3%)
    pallas_call x1, Pallas kernels, on_device(): pl.pallas_call(kernel, out_shape=(jax.ShapeDtypeStruct((ROWS, H), BF), ja...  78.8 us
    unnamed x2, local copies, waits for them, and re-layouts  2.59 us

profile of v2, /device:TPU:6, one launch (start us, length us, event | category | flops | bytes accessed | tf_op | source)
XLA Modules:
  0.0 82.0 jit_solution(12996788506276429648)
XLA Ops:
  0.6 78.8 %relational_layer.1 = (bf16[128,256]{1,0:T(8,128)(2,1)}, f32[1,32]{1,0:T(1,128)}) custom-call(bf16[1024,512]{1,0:T(8,128)(2,1)} %table.1, bf16[32,128,128]{2,1,0:T(8,128)(2,1)} %bitcast.3, s32[32,128]{1,0:T(8,128)} %bitcast.4, s32[16,2,128]{2,1,0:T(2,128)} %bitcast.5, s32[1,32]{1,0:T(1,128)} %mask_any.1, f32[1,32]{1,0:T(1,128)} %coef_any.1, ...), custom_call_target="tpu_custom_call" | custom-call | tf_op jit(solution)/shard_map/relational_layer/pallas_call | solution.py:331
  79.4 1.5 %copy.14 = bf16[128,256]{1,0:T(8,128)(2,1)} copy(bf16[128,256]{1,0:T(8,128)(2,1)} %get-tuple-element.4) | data formatting | bytes 131072
  80.9 1.1 %copy.15 = f32[1,32]{1,0:T(1,128)} copy(f32[1,32]{1,0:T(1,128)} %get-tuple-element.5) | data formatting | bytes 256

commit v3 on v2

--- a/solution.py
+++ b/solution.py
@@ -13,7 +13,8 @@
 TAB, F, H, BLK, ROWS, BASES = 1024, 512, 256, 128, 128, 32
 OWN = NR * ROWS
 CHUNK = 2 * BLK
-EARLY = 6
+NQ, Q = 2, 128
+EARLY = 3
 
 
 def offset(k):
@@ -27,8 +28,8 @@
     out, grad,
     mask, coef, type_rows, bias,
     tbl, edg, sid, bas, hot, sbuf, rbuf, ids, hot_t, acc, accb, acct, gbuf, wall, wbuf,
-    s_send, s_recv, s_all, z_sib, z_sibr, z_own, z_send, z_recv, part, p_send, p_recv,
-    load_sem, c_ss, c_rs, i_ss, i_rs, g_ss, g_rs, w_sem, s_sem, sib_ss, sib_rs, z_ss, z_rs, p_ss, p_rs,
+    s_send, s_recv, s_all, grad_sums, z_sib, z_sibr, z_own, z_send, z_recv, part, p_send, p_recv,
+    load_sem, c_ss, c_rs, i_ss, i_rs, g_ss, g_rs, w_sem, s_ss, s_rs, sib_ss, sib_rs, z_ss, z_rs, p_ss, p_rs,
 ):
     rel, dst, mp = lax.axis_index("rel"), lax.axis_index("dst"), lax.axis_index("mp")
     x, core = rel // NC, rel % NC
@@ -40,6 +41,20 @@
 
     def remote(src, to, ss, rs, **where):
         return pltpu.make_async_remote_copy(src, to, ss, rs, device_id=where, device_id_type=MESH)
+
+    barrier = pltpu.get_barrier_semaphore()
+    group = sorted(range(1, ND * NM), key=lambda q: abs(q - ND))
+    across = [(dx, dm) for dx in range(1, NX) for dm in range(NM)]
+
+    def greet(**where):
+        pl.semaphore_signal(barrier, inc=1, device_id=where, device_id_type=MESH)
+
+    for q in group:
+        greet(dst=(dst + q // NM) % ND, mp=(mp + q % NM) % NM)
+    for dx, dm in across:
+        greet(rel=(x + dx) % NX * NC + core, mp=(mp + dm) % NM)
+    sibling = x * NC + 1 - core
+    greet(rel=sibling)
 
     loads = [
         load(0, src_ids, sid),
@@ -56,23 +71,9 @@
     for copy in loads[:9]:
         copy.start()
 
-    barrier = pltpu.get_barrier_semaphore()
-    group = [q for q in range(1, ND * NM)]
-    across = [(dx, dm) for dx in range(1, NX) for dm in range(NM)]
-
-    def greet(**where):
-        pl.semaphore_signal(barrier, inc=1, device_id=where, device_id_type=MESH)
-
-    for q in group:
-        greet(dst=(dst + q // NM) % ND, mp=(mp + q % NM) % NM)
-    for dx, dm in across:
-        greet(rel=(x + dx) % NX * NC + core, mp=(mp + dm) % NM)
-    sibling = x * NC + 1 - core
-    greet(rel=sibling)
-
     lanes = lax.broadcasted_iota(jnp.int32, (BLK, BLK), 1)
 
-    def make_chunk(d, to):
+    def make_chunk(d, to, at):
         for half in range(2):
             k = 2 * d + half
             row = sid[pl.ds(k, 1), :]
@@ -86,9 +87,11 @@
             k = 2 * d + half
             live = mask[0, k].astype(F32)
             block = (edg[k].astype(F32) * live).astype(BF)
-            to[half * BLK : (half + 1) * BLK, :] = jnp.dot(
+            made = jnp.dot(
                 block, picked[half * BLK : (half + 1) * BLK, :], preferred_element_type=F32
             ).astype(BF)
+            for q in range(NQ):
+                to[q, at, half * BLK : (half + 1) * BLK, :] = made[:, q * Q : (q + 1) * Q]
 
     def peer(k, sign):
         dz, dy = offset(k)
@@ -100,17 +103,19 @@
     def id_copy(to):
         return remote(dst_ids.at[to], ids.at[dst], i_ss.at[to], i_rs.at[dst], dst=to)
 
-    def chunk_copy(to):
-        return remote(sbuf.at[to], rbuf.at[dst], c_ss.at[to], c_rs.at[dst], dst=to)
+    def chunk_copy(to, q):
+        return remote(sbuf.at[q, to], rbuf.at[q, dst], c_ss.at[q, to], c_rs.at[q, dst], dst=to)
 
     def make(i, _):
         to = peer(kth(i), 1)
-        make_chunk(to, sbuf.at[to])
+        make_chunk(to, sbuf, to)
         return 0
 
-    def send(i, _):
-        chunk_copy(peer(kth(i), 1)).start()
-        return 0
+    def send(q):
+        def start(i, _):
+            chunk_copy(peer(kth(i), 1), q).start()
+            return 0
+        return start
 
     def send_ids(i, _):
         id_copy(peer(kth(i), 1)).start()
@@ -118,7 +123,7 @@
 
     def make_send(i, _):
         make(i, 0)
-        return send(i, 0)
+        return send(0)(i, 0)
 
     for i in range(4):
         loads[i].wait()
@@ -126,14 +131,15 @@
     loads[4].wait()
     loads[5].wait()
     pl.semaphore_wait(barrier, len(group) + len(across) + 1)
-    lax.fori_loop(0, EARLY, send, 0)
+    lax.fori_loop(0, EARLY, send(0), 0)
     lax.fori_loop(0, ND - 1, send_ids, 0)
     mine = gbuf.at[core, mp, x]
     g_pair = remote(mine, mine, g_ss.at[0], g_rs.at[0], mp=other)
     g_pair.start()
     loads[9].start()
     lax.fori_loop(EARLY, ND - 1, make_send, 0)
-    make_chunk(dst, rbuf.at[dst])
+    lax.fori_loop(0, ND - 1, send(1), 0)
+    make_chunk(dst, rbuf, dst)
 
     g_pair.wait_recv()
 
@@ -165,25 +171,73 @@
     half_rows = NX * ROWS
     rows = ((place % half_rows) // ROWS * NC + place // half_rows) * ROWS + place % ROWS
 
-    def add_chunk(s):
+    def add_chunk(s, q):
         for half in range(2):
             row = ids[s, half : half + 1, :]
             hot_t[:, half * BLK : (half + 1) * BLK] = jnp.where(rows == row, 1.0, 0.0).astype(BF)
-        return jnp.dot(hot_t[...], rbuf[s], preferred_element_type=F32)
-
-    acc[...] = add_chunk(dst)
-
-    def take(i):
+        return jnp.dot(hot_t[...], rbuf[q, s], preferred_element_type=F32)
+
+    for q in range(NQ):
+        acc[q] = add_chunk(dst, q)
+
+    def take(i, q):
         s = peer(kth(i), -1)
-        remote(dst_ids.at[s], ids.at[s], i_ss.at[s], i_rs.at[s], dst=s).wait_recv()
-        remote(sbuf.at[s], rbuf.at[s], c_ss.at[s], c_rs.at[s], dst=s).wait_recv()
-        return add_chunk(s)
-
-    def take_chunk(i, _):
-        acc[...] += take(i)
-        return 0
-
-    lax.fori_loop(0, 8, take_chunk, 0)
+        if q == 0:
+            remote(dst_ids.at[s], ids.at[s], i_ss.at[s], i_rs.at[s], dst=s).wait_recv()
+        remote(sbuf.at[q, s], rbuf.at[q, s], c_ss.at[q, s], c_rs.at[q, s], dst=s).wait_recv()
+        return add_chunk(s, q)
+
+    def take_chunk(q):
+        def step(i, _):
+            acc[q] += take(i, q)
+            return 0
+        return step
+
+    def outer(g, q):
+        return jnp.dot(acct[q], gbuf[:, g].reshape(OWN, H), preferred_element_type=F32)
+
+    def s_copy(q):
+        return remote(s_send.at[q], s_recv.at[q], s_ss.at[q], s_rs.at[q], mp=other)
+
+    def s_rows(m, q):
+        return pl.multiple_of(m * H + q * Q, Q)
+
+    def sums_final(q, total):
+        half = total.astype(BF)
+        accb[:, q * Q : (q + 1) * Q] = half
+        acct[q] = half.T
+        s_send[q] = outer(other, q).astype(BF)
+        s_copy(q).start()
+
+    DT = 16
+
+    def against(m, q):
+        base = s_rows(m, q)
+        def step(t, sums):
+            at = pl.multiple_of(base + t * DT, DT)
+            s = s_all[pl.ds(at, DT), :]
+            new = []
+            for b in range(BASES):
+                v = bas[b, pl.ds(at, DT), :].astype(F32) * s
+                v = (v[0:8, 0:128] + v[8:16, 0:128]) + (v[0:8, 128:256] + v[8:16, 128:256])
+                new.append(sums[b] + v)
+            return tuple(new)
+        first = tuple(grad_sums[b] for b in range(BASES))
+        sums = lax.fori_loop(0, Q // DT, step, first)
+        for b in range(BASES):
+            grad_sums[b] = sums[b]
+
+    def against_own(q):
+        s_all[pl.ds(s_rows(mp, q), Q), :] = outer(mp, q)
+        against(mp, q)
+
+    def against_other(q):
+        s_copy(q).wait_recv()
+        s_all[pl.ds(s_rows(other, q), Q), :] = s_recv[q].astype(F32)
+        against(other, q)
+
+    grad_sums[...] = jnp.zeros_like(grad_sums)
+    lax.fori_loop(0, 4, take_chunk(0), 0)
 
     for dx in range(1, NX):
         theirs = gbuf.at[core, :, (x - dx + NX) % NX]
@@ -191,19 +245,16 @@
     g_sib = remote(gbuf.at[core], gbuf.at[core], g_ss.at[NX], g_rs.at[NX], rel=sibling)
     g_sib.start()
 
-    lax.fori_loop(8, ND - 2, take_chunk, 0)
+    lax.fori_loop(4, ND - 1, take_chunk(0), 0)
     g_sib.wait_recv()
+    sums_final(0, acc[0])
+    lax.fori_loop(0, 2, take_chunk(1), 0)
+    against_own(0)
+    lax.fori_loop(2, 6, take_chunk(1), 0)
+    against_other(0)
     w_copy.wait_recv()
-
-    accb[...] = (acc[...] + take(ND - 2)).astype(BF)
-    acct[...] = accb[...].T
-
-    def outer(g):
-        return jnp.dot(acct[...], gbuf[:, g].reshape(OWN, H), preferred_element_type=F32)
-
-    s_send[...] = outer(other).astype(BF)
-    s_copy = remote(s_send, s_recv, s_sem.at[0], s_sem.at[1], mp=other)
-    s_copy.start()
+    lax.fori_loop(6, ND - 2, take_chunk(1), 0)
+    sums_final(1, acc[1] + take(ND - 2, 1))
 
     def times_w(c, g):
         return jnp.dot(
@@ -240,28 +291,13 @@
             else:
                 z_recv[x * NM + mp] = piece
 
-    s_all[pl.ds(pl.multiple_of(mp * H, H), H), :] = outer(mp)
-    DT = 16
-
-    def against(base):
-        def step(t, sums):
-            at = pl.multiple_of(base + t * DT, DT)
-            s = s_all[pl.ds(at, DT), :]
-            new = []
-            for b in range(BASES):
-                v = bas[b, pl.ds(at, DT), :].astype(F32) * s
-                v = (v[0:8, 0:128] + v[8:16, 0:128]) + (v[0:8, 128:256] + v[8:16, 128:256])
-                new.append(sums[b] + v)
-            return tuple(new)
-        return step
-
-    zeros = tuple(jnp.zeros((8, 128), F32) for _ in range(BASES))
-    sums = lax.fori_loop(0, H // DT, against(mp * H), zeros)
+    against_own(1)
 
     def done_chunk(i, _):
         to = peer(kth(i), 1)
         id_copy(to).wait_send()
-        chunk_copy(to).wait_send()
+        for q in range(NQ):
+            chunk_copy(to, q).wait_send()
         return 0
 
     lax.fori_loop(0, ND - 1, done_chunk, 0)
@@ -271,11 +307,9 @@
     g_sib.wait_send()
     w_copy.wait_send()
 
-    s_copy.wait_recv()
-    s_all[pl.ds(pl.multiple_of(other * H, H), H), :] = s_recv[...].astype(F32)
-    sums = lax.fori_loop(0, H // DT, against(other * H), sums)
+    against_other(1)
     for b in range(BASES):
-        part[b : b + 1, :] = jnp.sum(sums[b], axis=0, keepdims=True)
+        part[b : b + 1, :] = jnp.sum(grad_sums[b], axis=0, keepdims=True)
     total = jnp.sum(part[...].T, axis=0, keepdims=True)
     me = dst * NM + mp
     p_send[...] = total
@@ -305,7 +339,8 @@
         total = total + z_recv[q].astype(F32)
     out[...] = (total + row_bias).astype(BF)
 
-    s_copy.wait_send()
+    for q in range(NQ):
+        s_copy(q).wait_send()
     for dm in (1, 0):
         sib_copy((mp + dm) % NM).wait_send()
     for dx, dm in across + [(0, 1)]:
@@ -346,19 +381,20 @@
             pltpu.VMEM((2 * ND, BLK), jnp.int32),
             pltpu.VMEM((BASES, F, H), BF),
             pltpu.VMEM((CHUNK, TAB), BF),
-            pltpu.VMEM((ND, CHUNK, H), BF),
-            pltpu.VMEM((ND, CHUNK, H), BF),
+            pltpu.VMEM((NQ, ND, CHUNK, Q), BF),
+            pltpu.VMEM((NQ, ND, CHUNK, Q), BF),
             pltpu.VMEM((ND, 2, BLK), jnp.int32),
             pltpu.VMEM((OWN, CHUNK), BF),
-            pltpu.VMEM((OWN, H), F32),
+            pltpu.VMEM((NQ, OWN, Q), F32),
             pltpu.VMEM((OWN, H), BF),
-            pltpu.VMEM((H, OWN), BF),
+            pltpu.VMEM((NQ, Q, OWN), BF),
             pltpu.VMEM((NC, NM, NX, ROWS, H), BF),
             pltpu.VMEM((F, H), BF),
             pltpu.VMEM((NM, H, H), BF),
-            pltpu.VMEM((H, H), BF),
-            pltpu.VMEM((H, H), BF),
+            pltpu.VMEM((NQ, Q, H), BF),
+            pltpu.VMEM((NQ, Q, H), BF),
             pltpu.VMEM((F, H), F32),
+            pltpu.VMEM((BASES, 8, 128), F32),
             pltpu.VMEM((NM, NX * ROWS, H), BF),
             pltpu.VMEM((NM, NX * ROWS, H), BF),
             pltpu.VMEM((NM, NX * ROWS, H), F32),
@@ -368,9 +404,9 @@
             pltpu.VMEM((1, BASES), F32),
             pltpu.VMEM((ND * NM, 1, BASES), F32),
             dma((10,)),
-            dma((ND,)), dma((ND,)), dma((ND,)), dma((ND,)),
+            dma((NQ, ND)), dma((NQ, ND)), dma((ND,)), dma((ND,)),
             dma((NX + 1,)), dma((NX + 1,)),
-            dma((2,)), dma((2,)), dma((NM,)), dma((NM,)),
+            dma((2,)), dma((NQ,)), dma((NQ,)), dma((NM,)), dma((NM,)),
             dma((NX * NM,)), dma((NX * NM,)),
             dma((ND * NM,)), dma((ND * NM,)),
         ],

time: 82.2 us -> 80.6 us (0.981)
  Pallas kernels: 78.8 us -> 77.1 us
    pallas_call x1, Pallas kernels: 78.8 us -> 77.1 us  [on_device(): pl.pallas_call(kernel, out_shape=(jax.ShapeDtypeStruct((ROWS, H), BF), ja...]
where the time goes in v3:
time: 80.6 us; the launch traced here: 80.3 us
  Pallas kernels  77.1 us (96%)
  local copies, waits for them, and re-layouts  2.59 us (3%)
    pallas_call x1, Pallas kernels, on_device(): pl.pallas_call(kernel, out_shape=(jax.ShapeDtypeStruct((ROWS, H), BF), ja...  77.1 us
    unnamed x2, local copies, waits for them, and re-layouts  2.59 us

profile of v3, /device:TPU:6, one launch (start us, length us, event | category | flops | bytes accessed | tf_op | source)
XLA Modules:
  0.0 80.3 jit_solution(9199802168312362536)
XLA Ops:
  0.6 77.1 %relational_layer.1 = (bf16[128,256]{1,0:T(8,128)(2,1)}, f32[1,32]{1,0:T(1,128)}) custom-call(bf16[1024,512]{1,0:T(8,128)(2,1)} %table.1, bf16[32,128,128]{2,1,0:T(8,128)(2,1)} %bitcast.3, s32[32,128]{1,0:T(8,128)} %bitcast.4, s32[16,2,128]{2,1,0:T(2,128)} %bitcast.5, s32[1,32]{1,0:T(1,128)} %mask_any.1, f32[1,32]{1,0:T(1,128)} %coef_any.1, ...), custom_call_target="tpu_custom_call" | custom-call | tf_op jit(solution)/shard_map/relational_layer/pallas_call | solution.py:366
  77.7 1.5 %copy.14 = bf16[128,256]{1,0:T(8,128)(2,1)} copy(bf16[128,256]{1,0:T(8,128)(2,1)} %get-tuple-element.4) | data formatting | bytes 131072
  79.2 1.1 %copy.15 = f32[1,32]{1,0:T(1,128)} copy(f32[1,32]{1,0:T(1,128)} %get-tuple-element.5) | data formatting | bytes 256

commit v4 on v3

--- a/solution.py
+++ b/solution.py
@@ -29,7 +29,7 @@
     mask, coef, type_rows, bias,
     tbl, edg, sid, bas, hot, sbuf, rbuf, ids, hot_t, acc, accb, acct, gbuf, wall, wbuf,
     s_send, s_recv, s_all, grad_sums, z_sib, z_sibr, z_own, z_send, z_recv, part, p_send, p_recv,
-    load_sem, c_ss, c_rs, i_ss, i_rs, g_ss, g_rs, w_sem, s_ss, s_rs, sib_ss, sib_rs, z_ss, z_rs, p_ss, p_rs,
+    load_sem, c_ss, c_rs, i_ss, i_rs, g_ss, g_rs, w_sem, s_ss, s_rs, sib_ss, sib_rs, z_ss, z_rs, p_ss, p_rs, word,
 ):
     rel, dst, mp = lax.axis_index("rel"), lax.axis_index("dst"), lax.axis_index("mp")
     x, core = rel // NC, rel % NC
@@ -51,8 +51,9 @@
 
     for q in group:
         greet(dst=(dst + q // NM) % ND, mp=(mp + q % NM) % NM)
-    for dx, dm in across:
-        greet(rel=(x + dx) % NX * NC + core, mp=(mp + dm) % NM)
+    near_x = (1, NX - 1)
+    for dx in near_x:
+        greet(rel=(x + dx) % NX * NC + core)
     sibling = x * NC + 1 - core
     greet(rel=sibling)
 
@@ -130,7 +131,14 @@
     lax.fori_loop(0, EARLY, make, 0)
     loads[4].wait()
     loads[5].wait()
-    pl.semaphore_wait(barrier, len(group) + len(across) + 1)
+    pl.semaphore_wait(barrier, len(group) + len(near_x) + 1)
+
+    def tell(level):
+        for dx in near_x:
+            pl.semaphore_signal(
+                word.at[level], inc=1, device_id={"rel": (x + dx) % NX * NC + core}, device_id_type=MESH)
+
+    tell(0)
     lax.fori_loop(0, EARLY, send(0), 0)
     lax.fori_loop(0, ND - 1, send_ids, 0)
     mine = gbuf.at[core, mp, x]
@@ -147,8 +155,11 @@
         both = gbuf.at[core, :, x]
         return remote(both, both, g_ss.at[dx], g_rs.at[dx], rel=(x + dx) % NX * NC + core)
 
+    pl.semaphore_wait(word.at[0], len(near_x))
+    tell(1)
     for dx in range(1, NX):
         g_across(dx).start()
+    pl.semaphore_wait(word.at[1], len(near_x))
 
     for i in (6, 7, 8, 9):
         loads[i].wait()
@@ -409,6 +420,7 @@
             dma((2,)), dma((NQ,)), dma((NQ,)), dma((NM,)), dma((NM,)),
             dma((NX * NM,)), dma((NX * NM,)),
             dma((ND * NM,)), dma((ND * NM,)),
+            pltpu.SemaphoreType.REGULAR((2,)),
         ],
         compiler_params=pltpu.CompilerParams(
             collective_id=0, has_side_effects=True, vmem_limit_bytes=67000000

time: 80.6 us -> 76.2 us (0.945)
  Pallas kernels: 77.1 us -> 72.8 us
    pallas_call x1, Pallas kernels: 77.1 us -> 72.8 us  [on_device(): pl.pallas_call(kernel, out_shape=(jax.ShapeDtypeStruct((ROWS, H), BF), ja...]
where the time goes in v4:
time: 76.2 us; the launch traced here: 76 us
  Pallas kernels  72.8 us (96%)
  local copies, waits for them, and re-layouts  2.59 us (3%)
    pallas_call x1, Pallas kernels, on_device(): pl.pallas_call(kernel, out_shape=(jax.ShapeDtypeStruct((ROWS, H), BF), ja...  72.8 us
    unnamed x2, local copies, waits for them, and re-layouts  2.59 us

profile of v4, /device:TPU:6, one launch (start us, length us, event | category | flops | bytes accessed | tf_op | source)
XLA Modules:
  0.0 76.0 jit_solution(9245411992137306643)
XLA Ops:
  0.6 72.8 %relational_layer.1 = (bf16[128,256]{1,0:T(8,128)(2,1)}, f32[1,32]{1,0:T(1,128)}) custom-call(bf16[1024,512]{1,0:T(8,128)(2,1)} %table.1, bf16[32,128,128]{2,1,0:T(8,128)(2,1)} %bitcast.3, s32[32,128]{1,0:T(8,128)} %bitcast.4, s32[16,2,128]{2,1,0:T(2,128)} %bitcast.5, s32[1,32]{1,0:T(1,128)} %mask_any.1, f32[1,32]{1,0:T(1,128)} %coef_any.1, ...), custom_call_target="tpu_custom_call" | custom-call | tf_op jit(solution)/shard_map/relational_layer/pallas_call | solution.py:377
  73.4 1.5 %copy.14 = bf16[128,256]{1,0:T(8,128)(2,1)} copy(bf16[128,256]{1,0:T(8,128)(2,1)} %get-tuple-element.4) | data formatting | bytes 131072
  74.9 1.1 %copy.15 = f32[1,32]{1,0:T(1,128)} copy(f32[1,32]{1,0:T(1,128)} %get-tuple-element.5) | data formatting | bytes 256

commit v5 on v4

--- a/solution.py
+++ b/solution.py
@@ -272,13 +272,22 @@
             accb[pl.ds(pl.multiple_of(c * half_rows, half_rows), half_rows), :], wbuf[g],
             preferred_element_type=F32)
 
-    def sib_copy(g):
-        return remote(z_sib.at[g], z_sibr.at[g], sib_ss.at[g], sib_rs.at[g], rel=sibling)
+    def z_rows(tx):
+        return pl.ds(pl.multiple_of(tx * ROWS, ROWS), ROWS)
+
+    def sib_copy(g, tx):
+        return remote(
+            z_sib.at[g, z_rows(tx)], z_sibr.at[g, z_rows(tx)], sib_ss.at[g, tx], sib_rs.at[g, tx], rel=sibling)
 
     columns = (other, mp)
+    order = (2, 1, 3, 0)
     for g in columns:
-        z_sib[g] = times_w(1 - core, g).astype(BF)
-        sib_copy(g).start()
+        for dx in order:
+            tx = (x + dx) % NX
+            first = pl.multiple_of((1 - core) * half_rows + tx * ROWS, ROWS)
+            z_sib[g, z_rows(tx), :] = jnp.dot(
+                accb[pl.ds(first, ROWS), :], wbuf[g], preferred_element_type=F32).astype(BF)
+            sib_copy(g, tx).start()
     for g in columns:
         z_own[g] = times_w(core, g)
 
@@ -288,13 +297,12 @@
             z_send.at[tm, tx], z_recv.at[x * NM + mp], z_ss.at[tx * NM + tm], z_rs.at[x * NM + mp],
             rel=tx * NC + core, mp=tm)
 
-    order = (2, 1, 3, 0)
     for dm in (1, 0):
         g = (mp + dm) % NM
-        sib_copy(g).wait_recv()
         for dx in order:
             tx = (x + dx) % NX
-            at = pl.ds(pl.multiple_of(tx * ROWS, ROWS), ROWS)
+            at = z_rows(tx)
+            sib_copy(g, tx).wait_recv()
             piece = (z_own[g, at, :] + z_sibr[g, at, :].astype(F32)).astype(BF)
             if dx or dm:
                 z_send[g, tx] = piece
@@ -339,21 +347,21 @@
     for c in range(1, 4):
         row_bias = jnp.where(at >= bound, bias[c : c + 1, :], row_bias)
         bound = bound + type_rows[c]
+    total = row_bias + z_recv[x * NM + mp].astype(F32)
     for dx, dm in across + [(0, 1)]:
         fx, fm = (x - dx + NX) % NX, (mp + dm) % NM
         slot = fx * NM + fm
         remote(
             z_send.at[fm, fx], z_recv.at[slot], z_ss.at[slot], z_rs.at[slot],
             rel=fx * NC + core, mp=fm).wait_recv()
-    total = z_recv[0].astype(F32)
-    for q in range(1, NX * NM):
-        total = total + z_recv[q].astype(F32)
-    out[...] = (total + row_bias).astype(BF)
+        total = total + z_recv[slot].astype(F32)
+    out[...] = total.astype(BF)
 
     for q in range(NQ):
         s_copy(q).wait_send()
     for dm in (1, 0):
-        sib_copy((mp + dm) % NM).wait_send()
+        for tx in range(NX):
+            sib_copy((mp + dm) % NM, tx).wait_send()
     for dx, dm in across + [(0, 1)]:
         z_copy(dx, dm).wait_send()
     for q in group:
@@ -417,7 +425,7 @@
             dma((10,)),
             dma((NQ, ND)), dma((NQ, ND)), dma((ND,)), dma((ND,)),
             dma((NX + 1,)), dma((NX + 1,)),
-            dma((2,)), dma((NQ,)), dma((NQ,)), dma((NM,)), dma((NM,)),
+            dma((2,)), dma((NQ,)), dma((NQ,)), dma((NM, NX)), dma((NM, NX)),
             dma((NX * NM,)), dma((NX * NM,)),
             dma((ND * NM,)), dma((ND * NM,)),
             pltpu.SemaphoreType.REGULAR((2,)),

time: 76.2 us -> 76.3 us (level)
  no operation moved by 1% of the time
where the time goes in v5:
time: 76.3 us; the launch traced here: 76.1 us
  Pallas kernels  72.9 us (96%)
  local copies, waits for them, and re-layouts  2.59 us (3%)
    pallas_call x1, Pallas kernels, on_device(): pl.pallas_call(kernel, out_shape=(jax.ShapeDtypeStruct((ROWS, H), BF), ja...  72.9 us
    unnamed x2, local copies, waits for them, and re-layouts  2.59 us

profile of v5, /device:TPU:6, one launch (start us, length us, event | category | flops | bytes accessed | tf_op | source)
XLA Modules:
  0.0 76.1 jit_solution(7478801756947958885)
XLA Ops:
  0.6 72.9 %relational_layer.1 = (bf16[128,256]{1,0:T(8,128)(2,1)}, f32[1,32]{1,0:T(1,128)}) custom-call(bf16[1024,512]{1,0:T(8,128)(2,1)} %table.1, bf16[32,128,128]{2,1,0:T(8,128)(2,1)} %bitcast.3, s32[32,128]{1,0:T(8,128)} %bitcast.4, s32[16,2,128]{2,1,0:T(2,128)} %bitcast.5, s32[1,32]{1,0:T(1,128)} %mask_any.1, f32[1,32]{1,0:T(1,128)} %coef_any.1, ...), custom_call_target="tpu_custom_call" | custom-call | tf_op jit(solution)/shard_map/relational_layer/pallas_call | solution.py:385
  73.5 1.5 %copy.14 = bf16[128,256]{1,0:T(8,128)(2,1)} copy(bf16[128,256]{1,0:T(8,128)(2,1)} %get-tuple-element.4) | data formatting | bytes 131072
  75.0 1.1 %copy.15 = f32[1,32]{1,0:T(1,128)} copy(f32[1,32]{1,0:T(1,128)} %get-tuple-element.5) | data formatting | bytes 256
